TPU v7x, 128 devices: a whole 4x4x4 slice. The times are simulated.
128 devices in a mesh: col: 4 (over y), blk: 32 (over x, z, core).
Axes of the slice: x: 4, y: 4, z: 4, core: 2. Of those that a mesh axis runs over, the one named last changes fastest.
Arguments:
- corner_up: bfloat16 [4, 256, 256], P('col'), may hold values from -0.375 to 0.375
- corner_dn: bfloat16 [4, 256, 256], P('col'), may hold values from -0.375 to 0.375
- edge_top: bfloat16 [4, 256, 36, 256], P('col', 'blk'), may hold values from -6 to 6
- edge_bot: bfloat16 [4, 256, 36, 256], P('col', 'blk'), may hold values from -6 to 6
- edge_up: bfloat16 [4, 256, 36, 256], P('col', 'blk'), may hold values from -0.375 to 0.375
- edge_dn: bfloat16 [4, 256, 36, 256], P('col', 'blk'), may hold values from -0.375 to 0.375
- site_up: bfloat16 [4, 36, 36, 36, 36], P('col'), may hold values from -0.15625 to 0.15625
- site_dn: bfloat16 [4, 36, 36, 36, 36], P('col'), may hold values from -0.15625 to 0.15625
- proj_up: bfloat16 [4, 9216, 256], P('col', 'blk'), may hold values from -0.0625 to 0.0625
- proj_dn: bfloat16 [4, 9216, 256], P('col', 'blk'), may hold values from -0.0625 to 0.0625
Outputs:
- half_proj: bfloat16 [4, 9216, 256], P('col', 'blk')
- next_up: bfloat16 [4, 256, 256], P('col', 'blk')
- next_dn: bfloat16 [4, 256, 256], P('col', 'blk')
All inputs are finite; a program needn't handle non-finite values.
Results may differ from a plain program's by a relative error of at most 0.018.
Values may be sent and summed in bfloat16 or wider, within the bound.
A program may use at most 128 MiB of HBM per device.

v0:
```python
import jax
import jax.numpy as jnp
from jax import lax
from jax.sharding import PartitionSpec as P


def sent_together(arrays, axis, dim, along):
    both = jnp.concatenate(arrays, axis=along)
    whole, at, done = (lax.all_gather(both, axis, axis=dim, tiled=True), 0, [])
    for a in arrays:
        done.append(lax.slice_in_dim(whole, at, at + a.shape[along], axis=along))
        at += a.shape[along]
    return tuple(done)


def in_blocks(x, dim, size):
    shape = x.shape
    parts = x.reshape(*shape[:dim], size, shape[dim] // size, *shape[dim + 1 :])
    return jnp.moveaxis(parts, dim, 0)


def summed_on_arrival(x, axis, dim):
    parts = in_blocks(x, dim, lax.axis_size(axis))
    arrived = lax.all_to_all(parts, axis, split_axis=0, concat_axis=0, tiled=True)
    return arrived.astype(jnp.float32).sum(axis=0)


def from_behind(value, axis, steps):
    count = lax.axis_size(axis)
    pairs = [(source, (source + steps) % count) for source in range(count)]
    return lax.ppermute(value, axis, pairs)


def enlarge(edge, grown, site):
    rows, width, chi = edge.shape
    wide = jnp.dot(
        edge.reshape(rows * width, chi), grown, preferred_element_type=jnp.float32
    ).astype(jnp.bfloat16)
    wide = wide.reshape(rows, width * width, chi)
    table = site.transpose(2, 1, 3, 0).reshape(width * width, width * width)

    def one_row(slab):
        return jnp.dot(table, slab, preferred_element_type=jnp.float32).astype(jnp.bfloat16)

    block = lax.map(one_row, wide)
    return block.reshape(rows * width, width * chi)


def per_device(
    corner_up, corner_dn, edge_top, edge_bot, edge_up, edge_dn, site_up, site_dn, proj_up, proj_dn
):
    upper_c = corner_up[0]
    lower_c = corner_dn[0]
    chi = upper_c.shape[0]
    width = edge_top.shape[2]
    own_rows = edge_up.shape[1]
    pieces = sent_together((edge_top[0], edge_bot[0]), "blk", 0, 1)
    count = pieces[0].shape[0]
    first = jnp.dot(
        upper_c, pieces[0].reshape(count, width * chi), preferred_element_type=jnp.float32
    )
    second = jnp.dot(
        lower_c, pieces[1].reshape(count, width * chi), preferred_element_type=jnp.float32
    )
    grown_up = first
    grown_dn = second
    grown_up = grown_up.astype(jnp.bfloat16)
    grown_dn = grown_dn.astype(jnp.bfloat16)
    quad_up = enlarge(edge_up[0], grown_up, site_up[0])
    quad_dn = enlarge(edge_dn[0], grown_dn, site_dn[0])
    lower_p = proj_dn[0]
    upper_p = proj_up[0]
    contract = (((0,), (0,)), ((), ()))
    scale = 1.0 / (chi * width) ** 0.5
    cut_full = lax.psum(
        lax.dot_general(quad_dn, lower_p, contract, preferred_element_type=jnp.float32).astype(
            jnp.bfloat16
        ),
        "blk",
    )
    half = jnp.dot(quad_up, cut_full, preferred_element_type=jnp.float32)
    half_proj = (half * scale).astype(jnp.bfloat16)
    index = lax.axis_index("blk")
    own_up = lax.dynamic_slice_in_dim(grown_up, index * own_rows, own_rows, 0).reshape(
        own_rows * width, chi
    )
    own_dn = lax.dynamic_slice_in_dim(grown_dn, index * own_rows, own_rows, 0).reshape(
        own_rows * width, chi
    )
    first = lax.dot_general(upper_p, own_up, contract, preferred_element_type=jnp.float32)
    second = lax.dot_general(lower_p, own_dn, contract, preferred_element_type=jnp.float32)
    fresh = summed_on_arrival(
        jnp.concatenate([first, second], axis=1).astype(jnp.bfloat16), "blk", 0
    ).astype(jnp.bfloat16)
    fresh_up = fresh[:, :chi]
    fresh_dn = fresh[:, chi:]
    moved_up, moved_dn = from_behind((fresh_up, fresh_dn), "col", 1)
    return (half_proj[None], moved_up[None], moved_dn[None])


def solution(mesh):
    in_specs = (
        P("col", None, None),
        P("col", None, None),
        P("col", "blk", None, None),
        P("col", "blk", None, None),
        P("col", "blk", None, None),
        P("col", "blk", None, None),
        P("col", None, None, None, None),
        P("col", None, None, None, None),
        P("col", "blk", None),
        P("col", "blk", None),
    )
    out_specs = (P("col", "blk", None), P("col", "blk", None), P("col", "blk", None))
    return jax.shard_map(
        per_device, mesh=mesh, in_specs=in_specs, out_specs=out_specs, check_vma=False
    )
```

profile of v0, /device:TPU:0, one launch (start us, length us, event | category | flops | bytes accessed | tf_op | source)
XLA Modules:
  0.0 335.3 jit_solution(16963341485698365643)
XLA Ops:
  10.1 20.9 %copy.28 = bf16[36,36,36,36]{3,2,1,0:T(8,128)(2,1)} copy(bf16[36,36,36,36]{2,0,1,3:T(8,128)(2,1)} %bitcast.91) | data formatting | bytes 6718464 | tf_op jit(solution)/shard_map/transpose | solution.py:40
  31.0 16.0 %reshape.47 = bf16[1296,1296]{1,0:T(8,128)(2,1)} reshape(bf16[36,36,36,36]{3,2,1,0:T(8,128)(2,1)} %copy.28) | data formatting | bytes 6718464 | tf_op jit(solution)/shard_map/reshape | solution.py:40
  47.0 21.2 %copy.25 = bf16[36,36,36,36]{3,2,1,0:T(8,128)(2,1)} copy(bf16[36,36,36,36]{2,0,1,3:T(8,128)(2,1)} %bitcast.92) | data formatting | bytes 6718464 | tf_op jit(solution)/shard_map/transpose | solution.py:40
  68.2 15.9 %reshape.43 = bf16[1296,1296]{1,0:T(8,128)(2,1)} reshape(bf16[36,36,36,36]{3,2,1,0:T(8,128)(2,1)} %copy.25) | data formatting | bytes 6718464 | tf_op jit(solution)/shard_map/reshape | solution.py:40
  84.1 11.1 %fusion.21 = (bf16[256,36,256]{2,1,0:T(8,128)(2,1)}, bf16[256,36,256]{2,1,0:T(8,128)(2,1)}) fusion(bf16[256,72,256]{2,1,0:T(8,128)(2,1)} %all-gather.2.cloned.1.call-done), kind=kLoop, calls=%fused_computation.37 | loop fusion | bytes 18874368 | tf_op jit(solution)/shard_map/slice | solution.py:11
  95.2 8.6 %copy.29 = bf16[256,36,256]{0,2,1:T(8,128)(2,1)} copy(bf16[256,36,256]{2,1,0:T(8,128)(2,1)} %get-tuple-element.66) | data formatting | bytes 9437184
  110.0 8.5 %copy.30 = bf16[256,36,256]{0,2,1:T(8,128)(2,1)} copy(bf16[256,36,256]{2,1,0:T(8,128)(2,1)} %get-tuple-element.65) | data formatting | bytes 9437184
  126.1 8.4 %all-to-all-start = ((bf16[32,8,512]{2,1,0:T(8,128)(2,1)}), bf16[32,8,512]{2,1,0:T(8,128)(2,1)S(1)}, u32[]{:S(2)}, u32[]{:S(2)}) async-start(bf16[32,8,512]{2,1,0:T(8,128)(2,1)} %pad_maximum_fusion.1), calls=%async_computation | async-start | bytes 524288 | tf_op jit(solution)/shard_map/all_to_all | solution.py:24
  134.6 6.3 %fusion.11 = bf16[288,9216]{1,0:T(8,128)(2,1)} fusion(bf16[288,256]{1,0:T(8,128)(2,1)S(1)} %reshape_squeeze.7, bf16[9216,256]{0,1:T(8,128)(2,1)} %copy-done.2), kind=kOutput, calls=%fused_computation.18 | convolution fusion | flops 1361608704 | bytes 10174464 | tf_op jit(solution)/shard_map/dot_general | solution.py:36
  140.8 11.7 %reshape.46 = bf16[8,1296,256]{2,1,0:T(8,128)(2,1)} reshape(bf16[288,9216]{1,0:T(8,128)(2,1)} %fusion.11) | data formatting | bytes 10616832 | tf_op jit(solution)/shard_map/reshape | solution.py:39
  155.3 34.0 %while.21 = (s32[]{:T(128)}, bf16[8,1296,256]{2,1,0:T(8,128)(2,1)}, bf16[8,1296,256]{2,1,0:T(8,128)(2,1)}, bf16[1296,1296]{1,0:T(8,128)(2,1)}, s32[]{:T(128)}) while((s32[]{:T(128)}, bf16[8,1296,256]{2,1,0:T(8,128)(2,1)}, bf16[8,1296,256]{2,1,0:T(8,128)(2,1)}, bf16[1296,1296]{1,0:T(8,128)(2,1)}, s32[]{:T(128)}) %tuple.41), condition=%wide.region_3.4_spmd, body=%wide.region_2.3_spmd.sunk | while | flops 860295168 | bytes 4977725 | solution.py:45
  172.2 4.3 %fusion.47 = bf16[8,1296,256]{2,1,0:T(8,128)(2,1)} fusion(bf16[8,1296,256]{2,1,0:T(8,128)(2,1)} %get-tuple-element.142, s32[]{:T(128)} %get-tuple-element.141, bf16[1296,1296]{1,0:T(8,128)(2,1)} %get-tuple-element.149, bf16[8,1296,256]{2,1,0:T(8,128)(2,1)} %get-tuple-element.148), kind=kOutput, calls=%fused_computation.8.clone.1 | convolution fusion | flops 860295168 | bytes 4977664 | tf_op jit(solution)/shard_map/while/body/eval_jaxpr/dot_general | solution.py:43
  189.3 10.4 %reshape.48 = bf16[288,9216]{1,0:T(8,128)(2,1)} reshape(bf16[8,1296,256]{2,1,0:T(8,128)(2,1)} %get-tuple-element.48) | data formatting | bytes 10616832 | tf_op jit(solution)/shard_map/reshape | solution.py:46
  199.7 7.3 %convolution_convert_fusion.4 = bf16[9216,256]{1,0:T(8,128)(2,1)} fusion(bf16[288,9216]{1,0:T(8,128)(2,1)} %reshape.48, bf16[1,288,256]{2,1,0:T(8,128)(2,1)S(1)} %copy-done), kind=kOutput, calls=%fused_computation.14 | convolution fusion | flops 1361313792 | bytes 10174464 | tf_op jit(solution)/shard_map/dot_general | solution.py:76
  207.0 6.3 %fusion.10 = bf16[288,9216]{1,0:T(8,128)(2,1)} fusion(bf16[288,256]{1,0:T(8,128)(2,1)S(1)} %reshape_squeeze.6, bf16[9216,256]{0,1:T(8,128)(2,1)} %copy-done.1), kind=kOutput, calls=%fused_computation.17 | convolution fusion | flops 1361608704 | bytes 10174464 | tf_op jit(solution)/shard_map/dot_general | solution.py:36
  213.3 11.7 %reshape.42 = bf16[8,1296,256]{2,1,0:T(8,128)(2,1)} reshape(bf16[288,9216]{1,0:T(8,128)(2,1)} %fusion.10) | data formatting | bytes 10616832 | tf_op jit(solution)/shard_map/reshape | solution.py:39
  230.9 34.4 %while.20 = (s32[]{:T(128)}, bf16[8,1296,256]{2,1,0:T(8,128)(2,1)}, bf16[8,1296,256]{2,1,0:T(8,128)(2,1)}, bf16[1296,1296]{1,0:T(8,128)(2,1)}, s32[]{:T(128)}) while((s32[]{:T(128)}, bf16[8,1296,256]{2,1,0:T(8,128)(2,1)}, bf16[8,1296,256]{2,1,0:T(8,128)(2,1)}, bf16[1296,1296]{1,0:T(8,128)(2,1)}, s32[]{:T(128)}) %tuple.38), condition=%wide.region_1.2_spmd, body=%wide.region_0.1_spmd.sunk | while | flops 860295168 | bytes 4977725 | solution.py:45
  230.9 4.3 %fusion.44 = bf16[8,1296,256]{2,1,0:T(8,128)(2,1)} fusion(bf16[8,1296,256]{2,1,0:T(8,128)(2,1)} %get-tuple-element.127, s32[]{:T(128)} %get-tuple-element.126, bf16[1296,1296]{1,0:T(8,128)(2,1)} %get-tuple-element.134, bf16[8,1296,256]{2,1,0:T(8,128)(2,1)} %get-tuple-element.133), kind=kOutput, calls=%fused_computation.2.clone.1 | convolution fusion | flops 860295168 | bytes 4977664 | tf_op jit(solution)/shard_map/while/body/eval_jaxpr/dot_general | solution.py:43
  235.2 4.4 %fusion.44 = bf16[8,1296,256]{2,1,0:T(8,128)(2,1)} fusion(bf16[8,1296,256]{2,1,0:T(8,128)(2,1)} %get-tuple-element.127, s32[]{:T(128)} %get-tuple-element.126, bf16[1296,1296]{1,0:T(8,128)(2,1)} %get-tuple-element.134, bf16[8,1296,256]{2,1,0:T(8,128)(2,1)} %get-tuple-element.133), kind=kOutput, calls=%fused_computation.2.clone.1 | convolution fusion | flops 860295168 | bytes 4977664 | tf_op jit(solution)/shard_map/while/body/eval_jaxpr/dot_general | solution.py:43
  239.6 4.3 %fusion.44 = bf16[8,1296,256]{2,1,0:T(8,128)(2,1)} fusion(bf16[8,1296,256]{2,1,0:T(8,128)(2,1)} %get-tuple-element.127, s32[]{:T(128)} %get-tuple-element.126, bf16[1296,1296]{1,0:T(8,128)(2,1)} %get-tuple-element.134, bf16[8,1296,256]{2,1,0:T(8,128)(2,1)} %get-tuple-element.133), kind=kOutput, calls=%fused_computation.2.clone.1 | convolution fusion | flops 860295168 | bytes 4977664 | tf_op jit(solution)/shard_map/while/body/eval_jaxpr/dot_general | solution.py:43
  248.2 4.3 %fusion.44 = bf16[8,1296,256]{2,1,0:T(8,128)(2,1)} fusion(bf16[8,1296,256]{2,1,0:T(8,128)(2,1)} %get-tuple-element.127, s32[]{:T(128)} %get-tuple-element.126, bf16[1296,1296]{1,0:T(8,128)(2,1)} %get-tuple-element.134, bf16[8,1296,256]{2,1,0:T(8,128)(2,1)} %get-tuple-element.133), kind=kOutput, calls=%fused_computation.2.clone.1 | convolution fusion | flops 860295168 | bytes 4977664 | tf_op jit(solution)/shard_map/while/body/eval_jaxpr/dot_general | solution.py:43
  265.3 10.4 %reshape.44 = bf16[288,9216]{1,0:T(8,128)(2,1)} reshape(bf16[8,1296,256]{2,1,0:T(8,128)(2,1)} %get-tuple-element.47) | data formatting | bytes 10616832 | tf_op jit(solution)/shard_map/reshape | solution.py:46
  275.7 45.5 %all-reduce.2.cloned.1.call-done = bf16[9216,256]{1,0:T(8,128)(2,1)} async-done(((bf16[9216,256]{1,0:T(8,128)(2,1)}), bf16[9216,256]{1,0:T(8,128)(2,1)}) %all-reduce.2.cloned.1.call-update) | async-done | bytes 4718608 | tf_op jit(solution)/shard_map/psum | solution.py:75
  321.2 6.1 %fusion.13 = bf16[1,288,256]{2,1,0:T(8,128)(2,1)} fusion(bf16[288,9216]{1,0:T(8,128)(2,1)} %reshape.44, bf16[9216,256]{1,0:T(8,128)(2,1)} %all-reduce.2.cloned.1.call-done), kind=kOutput, calls=%fused_computation.23 | convolution fusion | flops 1359101952 | bytes 10174464 | tf_op jit(solution)/shard_map/dot_general | solution.py:81
  (56 shorter events, 73.3 us)
Async XLA Ops:
  7.2 117.9 %copy-start = (bf16[1,288,256]{2,1,0:T(8,128)(2,1)S(1)}, bf16[1,288,256]{2,1,0:T(8,128)(2,1)}, u32[]{:S(2)}) copy-start(bf16[1,288,256]{2,1,0:T(8,128)(2,1)} %param.23) | copy-start | bytes 442372
  7.2 76.9 %all-gather.2.cloned.1.call-start = ((), (), s32[]{:S(2)}) async-start(), calls=%async_computation.1 | async-start | bytes 9732096 | tf_op jit(solution)/shard_map/all_gather | solution.py:9
  30.9 16.0 %copy-start.3 = (bf16[1,8,36,256]{3,1,2,0:T(8,128)(2,1)S(1)}, bf16[1,8,36,256]{3,1,2,0:T(8,128)(2,1)}, u32[]{:S(2)}) copy-start(bf16[1,8,36,256]{3,1,2,0:T(8,128)(2,1)} %param.18) | copy-start | bytes 442372
  95.2 8.6 %copy-start.5 = (bf16[1,256,256]{2,1,0:T(8,128)(2,1)S(1)}, bf16[1,256,256]{2,1,0:T(8,128)(2,1)}, u32[]{:S(2)}) copy-start(bf16[1,256,256]{2,1,0:T(8,128)(2,1)} %param.14) | copy-start | bytes 393220
  107.5 2.2 copy-start.1
  109.7 8.8 %copy-start.6 = (bf16[1,256,256]{2,1,0:T(8,128)(2,1)S(1)}, bf16[1,256,256]{2,1,0:T(8,128)(2,1)}, u32[]{:S(2)}) copy-start(bf16[1,256,256]{2,1,0:T(8,128)(2,1)} %param.15) | copy-start | bytes 393220
  118.5 6.2 %copy-start.4 = (bf16[1,288,256]{2,1,0:T(8,128)(2,1)S(1)}, bf16[1,288,256]{2,1,0:T(8,128)(2,1)}, u32[]{:S(2)}) copy-start(bf16[1,288,256]{2,1,0:T(8,128)(2,1)} %param.22) | copy-start | bytes 442372
  122.4 2.1 copy-start.2
  126.1 99.0 %all-to-all-start = ((bf16[32,8,512]{2,1,0:T(8,128)(2,1)}), bf16[32,8,512]{2,1,0:T(8,128)(2,1)S(1)}, u32[]{:S(2)}, u32[]{:S(2)}) async-start(bf16[32,8,512]{2,1,0:T(8,128)(2,1)} %pad_maximum_fusion.1), calls=%async_computation | async-start | bytes 524288 | tf_op jit(solution)/shard_map/all_to_all | solution.py:24
  134.5 186.7 %all-reduce.2.cloned.1.call-start = ((), (), s32[]{:S(2)}) async-start(), calls=%async_computation.2 | async-start | bytes 9437184 | tf_op jit(solution)/shard_map/psum | solution.py:75
  225.1 50.6 %collective-permute-start = (bf16[8,256]{1,0:T(8,128)(2,1)S(1)}, bf16[8,256]{1,0:T(8,128)(2,1)S(1)}, u32[]{:S(2)}, u32[]{:S(2)}) collective-permute-start(bf16[8,256]{1,0:T(8,128)(2,1)S(1)} %get-tuple-element.68), channel_id=1, source_target_pairs={{0,32},{32,64},{64,96},{96,0},{1,33},{33,65},{65,97},{97,1},{2,34}... | collective-permute-start | bytes 12296 | tf_op jit(solution)/shard_map/ppermute | solution.py:31
  226.6 49.0 %collective-permute-start.1 = (bf16[8,256]{1,0:T(8,128)(2,1)S(1)}, bf16[8,256]{1,0:T(8,128)(2,1)S(1)}, u32[]{:S(2)}, u32[]{:S(2)}) collective-permute-start(bf16[8,256]{1,0:T(8,128)(2,1)S(1)} %get-tuple-element.67), channel_id=1, source_target_pairs={{0,32},{32,64},{64,96},{96,0},{1,33},{33,65},{65,97},{97,1},{2,34}... | collective-permute-start | bytes 12296 | tf_op jit(solution)/shard_map/ppermute | solution.py:31
Sparse Core Ops, SparseCore 0:
  10.2 57.7 all-gather.1
  207.1 114.0 all-reduce.1
where the time goes:
time: 339 us; the launch traced here: 335 us
  local copies, waits for them, and re-layouts  160 us (47%)
  matrix products  102 us (30%)
  waiting for transfers between devices  45.5 us (13%)
  between operations  14.2 us (4%)
  starting transfers between devices  11.6 us (3%)
    dot_general x16, matrix products, one_row(): jnp.dot(table, slab, preferred_element_type=jnp.float32)  68.4 us
    psum x1, waiting for transfers between devices, per_device(): lax.psum(lax.dot_general(quad_dn, lower_p, contract, preferred_element_ty...  45.5 us
    transpose x2, local copies, waits for them, and re-layouts, enlarge(): table = site.transpose(2, 1, 3, 0).reshape(width * width, width * width)  42.1 us
    reshape x2, local copies, waits for them, and re-layouts, enlarge(): table = site.transpose(2, 1, 3, 0).reshape(width * width, width * width)  31.8 us
    unnamed x20, local copies, waits for them, and re-layouts  23.6 us
    reshape x2, local copies, waits for them, and re-layouts, enlarge(): wide = wide.reshape(rows, width * width, chi)  23.5 us
    reshape x2, local copies, waits for them, and re-layouts, enlarge(): return block.reshape(rows * width, width * chi)  20.7 us
    dot_general x2, matrix products, enlarge(): jnp.dot(edge.reshape(rows * width, chi), grown, preferred_element_type=jn...  12.6 us
  transfers between devices with their start and end apart: 5, of which 1 were waited for; matrix products, arithmetic and copies ran while one was open for 63% of the time, Pallas kernels for 0%

commit v1 on v0

v1 whole, which is shorter than its diff:
```python
import functools

import jax
import jax.numpy as jnp
from jax import lax
from jax.experimental import pallas as pl
from jax.experimental.pallas import tpu as pltpu
from jax.sharding import PartitionSpec as P

MESH = pl.DeviceIdType.MESH
BF = jnp.bfloat16
F32 = jnp.float32

CHI = 256
D = 36
DP = 40
NX = 4
NZ = 4
JW = 64
NU = 18
KT = 1536
TCH = 3
TROWS = 12 * DP
CW = 12 * JW


def low_lanes(shape):
    return lax.broadcasted_iota(jnp.int32, shape, len(shape) - 1) < 64


def swap_halves(a, b):
    low = low_lanes(a.shape)
    ra = pltpu.roll(a, 64, a.ndim - 1)
    rb = pltpu.roll(b, 64, b.ndim - 1)
    return jnp.where(low, a, rb), jnp.where(low, ra, b)


def kernel(
    cu, cd, et, eb, eu, ed, su, sd, pu, pd,
    half_out, nu_out, nd_out,
    send_e, e_all, rows, grown, grown_f, rows_f, table, stg, wk, qt, pt, p2,
    cp, cs, cb, cx, cf, hs, hr, fs, fr, fw, fn,
    stg_sem, ez_s, ez_r, ex_s, ex_r, eo_s, eo_r, rz_s, rz_r,
    c1_s, c1_r, c2_s, c2_r, c3_s, c3_r, c4_s, c4_r, h_s, h_r, f1_s, f1_r, f2_s, f2_r,
):
    col = lax.axis_index("col")
    blk = lax.axis_index("blk")
    x = blk // 8
    z = (blk // 2) % 4
    c = blk % 2
    cols = lax.axis_size("col")

    def dev(x_, z_, c_, col_=None):
        return (col if col_ is None else col_, (x_ * 4 + z_) * 2 + c_)

    def mod4(v):
        return (v + 8) % 4

    def rcopy(src, dst, ssem, rsem, device):
        return pltpu.make_async_remote_copy(
            src_ref=src, dst_ref=dst, send_sem=ssem, recv_sem=rsem, device_id=device, device_id_type=MESH
        )

    oc = 1 - c
    xp = [mod4(x + s) for s in range(4)]
    xm = [mod4(x - s) for s in range(4)]
    zp = [mod4(z + s) for s in range(4)]
    zm = [mod4(z - s) for s in range(4)]
    cnext = (col + 1) % cols
    cprev = (col + cols - 1) % cols

    sites = (sd, su)
    steps = [(k, q) for k in range(2) for q in range(6)]

    def site_copy(n):
        k, q = steps[n]
        return pltpu.make_async_copy(sites[k].at[pl.ds(6 * q, 6)], stg.at[n % 2], stg_sem.at[n % 2])

    site_copy(0).start()
    site_copy(1).start()

    bar = pltpu.get_barrier_semaphore()
    peers = [dev(x, z, oc)]
    for s in (1, 2, 3):
        peers += [dev(xp[s], z, c), dev(xp[s], z, oc), dev(x, zp[s], c)]
    for p_ in peers + [dev(x, z_, c, cprev) for z_ in range(4)]:
        pl.semaphore_signal(bar, inc=1, device_id=p_, device_id_type=MESH)

    for k, src in enumerate((eb, et)):
        v = src[...].astype(F32).reshape(NU, 2, 8, CHI)
        for h in range(2):
            a = v[:, 0, :, 128 * h : 128 * h + 128].reshape(NU * 8, 128)
            b = v[:, 1, :, 128 * h : 128 * h + 128].reshape(NU * 8, 128)
            lo, hi = swap_halves(a, b)
            send_e[k, 2 * h] = lo.astype(BF).reshape(NU, 8, 128)
            send_e[k, 2 * h + 1] = hi.astype(BF).reshape(NU, 8, 128)
        e_all[k, x, c, z] = send_e[k, z]

    zero4 = jnp.zeros((DP - D, CHI), F32)
    for kind, src in enumerate((ed, pd, eu, pu)):
        v = src[...].astype(F32)
        if kind % 2 == 0:
            v = v.reshape(8 * D, CHI)
        for h in range(2):
            rows_f[h, 0 : 8 * D] = v[:, 128 * h : 128 * h + 128]
        for i in range(8):
            at = pl.ds(i, D, stride=8) if kind % 2 == 0 else pl.ds(D * i, D)
            piece = jnp.concatenate([rows_f[h, at, :] for h in range(2)], axis=1)
            rows[kind, z, i] = jnp.concatenate([piece, zero4], axis=0).astype(BF)

    pl.semaphore_wait(bar, 14)

    def ez(k, s):
        return rcopy(send_e.at[k, zp[s]], e_all.at[k, x, c, z], ez_s.at[k, s], ez_r.at[k, s], dev(x, zp[s], c))

    def ez_in(k, s):
        return rcopy(send_e.at[k, zm[s]], e_all.at[k, x, c, zm[s]], ez_s.at[k, s], ez_r.at[k, s], dev(x, zm[s], c))

    def rz(kind, s):
        return rcopy(rows.at[kind, z], rows.at[kind, z], rz_s.at[kind, s], rz_r.at[kind, s], dev(x, zp[s], c))

    def rz_in(kind, s):
        return rcopy(rows.at[kind, zm[s]], rows.at[kind, zm[s]], rz_s.at[kind, s], rz_r.at[kind, s], dev(x, zm[s], c))

    for k in range(2):
        for s in (1, 3, 2):
            ez(k, s).start()
    for kind in range(4):
        for s in (1, 3, 2):
            rz(kind, s).start()

    def make_table(n):
        k, q = steps[n]
        site_copy(n).wait()

        def body(tp, carry):
            row = pl.multiple_of(80 * tp, 16)
            for h in range(2):
                parts = []
                for t in range(2):
                    v = [stg[n % 2, 3 * h + w, 2 * tp + t].astype(F32) for w in range(3)]
                    gap = jnp.zeros((D, 4), F32)
                    wide = jnp.concatenate([v[0], gap, v[1], gap, v[2], jnp.zeros((D, 12), F32)], axis=1)
                    parts += [wide, jnp.zeros((4, 128), F32)]
                table[k, pl.ds(row, 80), 256 * q + 128 * h : 256 * q + 128 * h + 128] = jnp.concatenate(
                    parts, axis=0
                ).astype(BF)
            return carry

        lax.fori_loop(0, 18, body, 0)
        if n + 2 < len(steps):
            site_copy(n + 2).start()

    def ex(k, s):
        ref = e_all.at[k, x, c]
        return rcopy(ref, ref, ex_s.at[k, s], ex_r.at[k, s], dev(xp[s], z, c))

    def ex_in(k, s):
        ref = e_all.at[k, xm[s], c]
        return rcopy(ref, ref, ex_s.at[k, s], ex_r.at[k, s], dev(xm[s], z, c))

    def eo(k, s):
        ref = e_all.at[k, xm[s], c]
        return rcopy(ref, ref, eo_s.at[k, s], eo_r.at[k, s], dev(x, z, oc))

    def eo_in(k, s):
        ref = e_all.at[k, xm[s], oc]
        return rcopy(ref, ref, eo_s.at[k, s], eo_r.at[k, s], dev(x, z, oc))

    make_table(0)
    make_table(1)
    for k in range(2):
        for s in (1, 3, 2):
            ez_in(k, s).wait_recv()
        for s in (1, 3, 2):
            ex(k, s).start()
        eo(k, 0).start()
    for n in range(2, 9):
        make_table(n)
    for s in (1, 3, 2):
        ex_in(0, s).wait_recv()
        eo(0, s).start()
    for n in range(9, 12):
        make_table(n)
    for s in (0, 1, 3, 2):
        eo_in(0, s).wait_recv()

    def grow(k, corner):
        cv = corner[...]

        def body(m, carry):
            halves = []
            for w in range(2):
                parts = [
                    e_all[k, x_, c_, z_, 2 * m + w].astype(F32) for x_ in range(4) for z_ in range(4) for c_ in range(2)
                ]
                halves.append(jnp.concatenate(parts, axis=0))
            e = jnp.concatenate(halves, axis=1).astype(BF)
            g = jnp.dot(cv, e, preferred_element_type=F32)
            grown_f[:, pl.ds(pl.multiple_of(256 * m, 256), 256)] = g
            grown[:, pl.ds(pl.multiple_of(256 * m, 256), 256)] = g.astype(BF)
            return carry

        lax.fori_loop(0, 9, body, 0)

    def fresh(k):
        kind = 1 + 2 * k
        v = rows[kind].astype(F32).reshape(32 * DP, CHI)
        for h in range(2):
            rows_f[h] = v[:, 128 * h : 128 * h + 128]
        gparts = []
        for u in range(D):
            for h in range(2):
                p2[32 * u : 32 * u + 32, 128 * h : 128 * h + 128] = rows_f[h, pl.ds(u, 32, stride=DP), :].astype(BF)
        for m in range(NU):
            g = jnp.concatenate(
                [
                    grown_f[pl.ds(pl.multiple_of(64 * x + 16 * z_ + 8 * c, 8), 8), 128 * m : 128 * m + 128]
                    for z_ in range(4)
                ],
                axis=0,
            )
            gparts += [g, pltpu.roll(g, 64, 1)]
        g2 = jnp.concatenate(gparts, axis=0).astype(BF)
        return lax.dot_general(p2[...], g2, (((0,), (0,)), ((), ())), preferred_element_type=F32)

    def widen(k):
        kind = 2 * k

        def body(g, carry):
            left = rows[kind, g // 2, pl.ds(4 * (g % 2), 4)].astype(F32).reshape(4 * DP, CHI).astype(BF)
            for qq in range(3):
                w = jnp.dot(left, grown[:, 768 * qq : 768 * qq + 768], preferred_element_type=F32)
                for ip in range(2):
                    us = []
                    for m in range(6):
                        a = w[80 * ip : 80 * ip + 40, 128 * m : 128 * m + 128]
                        b = w[80 * ip + 40 : 80 * ip + 80, 128 * m : 128 * m + 128]
                        us += list(swap_halves(a, b))
                    for h in range(4):
                        blockv = jnp.concatenate(us[3 * h : 3 * h + 3] + [jnp.zeros((8, 128), F32)], axis=0)
                        row = 512 * qq + 128 * h
                        wk[g, row : row + 128, 128 * ip : 128 * ip + 128] = blockv.astype(BF)
            return carry

        lax.fori_loop(0, 8, body, 0)

    def quad(k, ch):
        def body(g, carry):
            qv = jnp.dot(
                table[k, TROWS * ch : TROWS * ch + TROWS, :], wk[g], preferred_element_type=F32
            )
            for tp in range(6):
                for ip in range(2):
                    a = qv[80 * tp : 80 * tp + 40, 128 * ip : 128 * ip + 128]
                    b = qv[80 * tp + 40 : 80 * tp + 80, 128 * ip : 128 * ip + 128]
                    o0, o1 = swap_halves(a, b)
                    lane = CW * ch + 128 * tp
                    qt[pl.ds(pl.multiple_of(160 * g + 80 * ip, 16), 80), lane : lane + 128] = jnp.concatenate(
                        [o0, o1], axis=0
                    ).astype(BF)
            return carry

        lax.fori_loop(0, 8, body, 0)

    grow(0, cd)
    for s in (1, 3, 2):
        rz_in(0, s).wait_recv()
    for s in (1, 3, 2):
        rz_in(1, s).wait_recv()
    fresh_dn = fresh(0)
    fw[...] = fresh_dn
    for h in range(2):
        pt[128 * h : 128 * h + 128, :] = rows_f[h].T.astype(BF)
    widen(0)
    for s in (1, 3, 2):
        ex_in(1, s).wait_recv()
        eo(1, s).start()

    def c1(ch):
        return rcopy(cp.at[ch, oc], cs.at[ch], c1_s.at[ch], c1_r.at[ch], dev(x, z, oc))

    def c2(ch, s):
        return rcopy(cb.at[ch, xp[s]], cx.at[ch, s], c2_s.at[ch, s], c2_r.at[ch, s], dev(xp[s], z, c))

    def c3(ch, s):
        ref = cf.at[ch, c, x]
        return rcopy(ref, ref, c3_s.at[ch, s], c3_r.at[ch, s], dev(xp[s], z, c))

    def c3_in(ch, s):
        ref = cf.at[ch, c, xm[s]]
        return rcopy(ref, ref, c3_s.at[ch, s], c3_r.at[ch, s], dev(xm[s], z, c))

    def c4(ch):
        ref = cf.at[ch, c]
        return rcopy(ref, ref, c4_s.at[ch], c4_r.at[ch], dev(x, z, oc))

    def c4_in(ch):
        ref = cf.at[ch, oc]
        return rcopy(ref, ref, c4_s.at[ch], c4_r.at[ch], dev(x, z, oc))

    def cut1(ch):
        part = jnp.dot(pt[...], qt[:, CW * ch : CW * ch + CW], preferred_element_type=F32).astype(BF)
        cp[ch] = part.reshape(2, 128, CW)
        c1(ch).start()

    def cut2(ch):
        c1(ch).wait_recv()
        both = cp[ch, c].astype(F32) + cs[ch].astype(F32)
        cb[ch] = both.astype(BF).reshape(4, 32, CW)
        for s in (1, 3, 2):
            c2(ch, s).start()

    def cut3(ch):
        for s in (1, 3, 2):
            c2(ch, s).wait_recv()
        total = cb[ch, x].astype(F32)
        for s in (1, 2, 3):
            total = total + cx[ch, s].astype(F32)
        cf[ch, c, x] = total.astype(BF)
        for s in (1, 3, 2):
            c3(ch, s).start()

    def cut4(ch):
        for s in (1, 3, 2):
            c3_in(ch, s).wait_recv()
        c4(ch).start()

    quad(0, 0)
    cut1(0)
    quad(0, 1)
    cut1(1)
    cut2(0)
    quad(0, 2)
    cut1(2)
    cut2(1)
    cut3(0)

    for s in (0, 1, 3, 2):
        eo_in(1, s).wait_recv()
    grow(1, cu)
    for s in (1, 3, 2):
        rz_in(3, s).wait_recv()
    fresh_up = fresh(1)
    both = jnp.where(low_lanes((CHI, 128)), fw[...], pltpu.roll(fresh_up, 64, 1))
    for x_ in range(4):
        for z_ in range(4):
            for c_ in range(2):
                at = 64 * x_ + 16 * z_ + 8 * c_
                fs[2 * x_ + c_, z_] = both[at : at + 8]
    me = 2 * x + c

    def f1_pairs():
        out = []
        for s in range(4):
            for o in range(2):
                if s or o:
                    out.append((2 * s + o, 2 * xp[s] + (oc if o else c), dev(xp[s], z, oc if o else c)))
        return out

    def f1(n, to, device):
        return rcopy(fs.at[to], fr.at[n], f1_s.at[n], f1_r.at[n], device)

    for a in f1_pairs():
        f1(*a).start()
    cut2(2)
    cut3(1)
    for s in (1, 3, 2):
        rz_in(2, s).wait_recv()
    widen(1)
    cut3(2)
    cut4(0)
    quad(1, 0)
    cut4(1)

    def f2(z_):
        return rcopy(fr.at[0, z_], fn.at[z], f2_s.at[z_], f2_r.at[z], dev(x, z_, c, cnext))

    def f2_in(z_):
        return rcopy(fr.at[0, z_], fn.at[z_], f2_s.at[z_], f2_r.at[z_], dev(x, z_, c, cnext))

    for a in f1_pairs():
        f1(*a).wait_recv()
    total = fs[me]
    for n in range(1, 8):
        total = total + fr[n]
    fr[0] = total
    for z_ in range(4):
        f2(z_).start()
    quad(1, 1)
    cut4(2)
    quad(1, 2)

    for ch in range(TCH):
        c4_in(ch).wait_recv()

    def h1(s):
        return rcopy(hs.at[zp[s]], hr.at[s], h_s.at[s], h_r.at[s], dev(x, zp[s], c))

    scale = 1.0 / (CHI * D) ** 0.5

    def half_of(z_):
        acc = None
        for ch in range(TCH):
            left = qt[pl.ds(pl.multiple_of(320 * z_, 320), 320), CW * ch : CW * ch + CW]
            right = cf[ch].reshape(CHI, CW)
            t = lax.dot_general(left, right, (((1,), (1,)), ((), ())), preferred_element_type=F32)
            acc = t if acc is None else acc + t
        return acc * scale

    for s in (2, 1, 3):
        hs[zp[s]] = half_of(zp[s]).astype(BF)
        h1(s).start()
    acc = half_of(z)
    for z_ in range(4):
        f2_in(z_).wait_recv()
    lo, hi = swap_halves(fn[0], fn[1])
    lo2, hi2 = swap_halves(fn[2], fn[3])
    nd_out[:, 0:128] = lo.astype(BF)
    nd_out[:, 128:256] = lo2.astype(BF)
    nu_out[:, 0:128] = hi.astype(BF)
    nu_out[:, 128:256] = hi2.astype(BF)
    for s in (1, 3, 2):
        h1(s).wait_recv()
        acc = acc + hr[s].astype(F32)
    half_out[...] = acc.reshape(8, DP, CHI)[:, :D].astype(BF)

    for k in range(2):
        for s in (1, 2, 3):
            ez(k, s).wait_send()
            ex(k, s).wait_send()
        for s in range(4):
            eo(k, s).wait_send()
    for kind in range(4):
        for s in (1, 2, 3):
            rz(kind, s).wait_send()
    for ch in range(TCH):
        c1(ch).wait_send()
        for s in (1, 2, 3):
            c2(ch, s).wait_send()
            c3(ch, s).wait_send()
        c4(ch).wait_send()
    for s in (1, 2, 3):
        h1(s).wait_send()
    for a in f1_pairs():
        f1(*a).wait_send()
    for z_ in range(4):
        f2(z_).wait_send()


def per_device(cu, cd, et, eb, eu, ed, su, sd, pu, pd):
    vmem = pl.BlockSpec(memory_space=pltpu.VMEM)
    hbm = pl.BlockSpec(memory_space=pl.ANY)
    dma = pltpu.SemaphoreType.DMA
    scratch = [
        pltpu.VMEM((2, 4, NU, 8, 128), BF),
        pltpu.VMEM((2, 4, 2, 4, NU, 8, 128), BF),
        pltpu.VMEM((4, 4, 8, DP, CHI), BF),
        pltpu.VMEM((CHI, D * JW), BF),
        pltpu.VMEM((CHI, D * JW), F32),
        pltpu.VMEM((2, 32 * DP, 128), F32),
        pltpu.VMEM((2, D * DP, KT), BF),
        pltpu.VMEM((2, 6, D, D, D), BF),
        pltpu.VMEM((8, KT, 256), BF),
        pltpu.VMEM((32 * DP, D * JW), BF),
        pltpu.VMEM((CHI, 32 * DP), BF),
        pltpu.VMEM((D * 32, CHI), BF),
        pltpu.VMEM((TCH, 2, 128, CW), BF),
        pltpu.VMEM((TCH, 128, CW), BF),
        pltpu.VMEM((TCH, 4, 32, CW), BF),
        pltpu.VMEM((TCH, 4, 32, CW), BF),
        pltpu.VMEM((TCH, 2, 4, 32, CW), BF),
        pltpu.VMEM((4, 8 * DP, CHI), BF),
        pltpu.VMEM((4, 8 * DP, CHI), BF),
        pltpu.VMEM((8, 4, 8, 128), F32),
        pltpu.VMEM((8, 4, 8, 128), F32),
        pltpu.VMEM((CHI, 128), F32),
        pltpu.VMEM((4, 8, 128), F32),
        dma((2,)),
        dma((2, 4)), dma((2, 4)),
        dma((2, 4)), dma((2, 4)),
        dma((2, 4)), dma((2, 4)),
        dma((4, 4)), dma((4, 4)),
        dma((TCH,)), dma((TCH,)),
        dma((TCH, 4)), dma((TCH, 4)),
        dma((TCH, 4)), dma((TCH, 4)),
        dma((TCH,)), dma((TCH,)),
        dma((4,)), dma((4,)),
        dma((8,)), dma((8,)),
        dma((4,)), dma((4,)),
    ]
    swap = lambda e: jnp.transpose(e[0], (1, 0, 2))
    half, nu, nd = pl.pallas_call(
        kernel,
        out_shape=(
            jax.ShapeDtypeStruct((8, D, CHI), BF),
            jax.ShapeDtypeStruct((8, CHI), BF),
            jax.ShapeDtypeStruct((8, CHI), BF),
        ),
        in_specs=[vmem] * 6 + [hbm] * 2 + [vmem] * 2,
        out_specs=(vmem,) * 3,
        scratch_shapes=scratch,
        compiler_params=pltpu.CompilerParams(
            collective_id=0, has_side_effects=True, vmem_limit_bytes=62 * 1024 * 1024
        ),
        name="ctm_step",
    )(cu[0], cd[0], swap(et), swap(eb), swap(eu), swap(ed), su[0], sd[0], pu[0], pd[0])
    return half.reshape(1, 8 * D, CHI), nu[None], nd[None]


def solution(mesh):
    in_specs = (
        P("col", None, None),
        P("col", None, None),
        P("col", "blk", None, None),
        P("col", "blk", None, None),
        P("col", "blk", None, None),
        P("col", "blk", None, None),
        P("col", None, None, None, None),
        P("col", None, None, None, None),
        P("col", "blk", None),
        P("col", "blk", None),
    )
    out_specs = (P("col", "blk", None), P("col", "blk", None), P("col", "blk", None))
    return jax.shard_map(
        per_device, mesh=mesh, in_specs=in_specs, out_specs=out_specs, check_vma=False
    )
```

time: 339 us -> 95.4 us (0.28); the launches traced: 335 us -> 95.2 us
  local copies, waits for them, and re-layouts: 160 us -> 4.14 us
  matrix products: 102 us -> 0 us
  Pallas kernels: 0 us -> 90.4 us
  waiting for transfers between devices: 45.5 us -> 0 us
  between operations: 14.2 us -> 0.64 us
  starting transfers between devices: 11.6 us -> 0 us
    dot_general x24 -> x0, matrix products: 102 us -> none  [the longest x16 68.4 us: one_row(): jnp.dot(table, slab, preferred_element_type=jnp.float32)]
    pallas_call x0 -> x1, Pallas kernels: none -> 90.4 us  [per_device(): pl.pallas_call(kernel, out_shape=(jax.ShapeDtypeStruct((8, D, CHI), BF),...]
    reshape x8 -> x1, local copies, waits for them, and re-layouts: 76.5 us -> 1.61 us  [per_device(): return (half.reshape(1, 8 * D, CHI), nu[None], nd[None])]
    psum x1 -> x0, waiting for transfers between devices: 45.5 us -> none  [per_device(): lax.psum(lax.dot_general(quad_dn, lower_p, contract, preferred_element_ty...]
    transpose x2 -> x0, local copies, waits for them, and re-layouts: 42.1 us -> none  [enlarge(): table = site.transpose(2, 1, 3, 0).reshape(width * width, width * width)]
    unnamed x20 -> x2, local copies, waits for them, and re-layouts: 23.6 us -> 2.54 us
    slice x2 -> x0, local copies, waits for them, and re-layouts: 11.1 us -> none  [the longest x1 11.1 us: sent_together(): done.append(lax.slice_in_dim(whole, at, at + a.shape[along], axis=along))]
    all_to_all x1 -> x0, starting transfers between devices: 8.45 us -> none  [summed_on_arrival(): lax.all_to_all(parts, axis, split_axis=0, concat_axis=0, tiled=True)]
  transfers between devices with their start and end apart: 5 -> 0, of which waited for: 1 -> 0; matrix products, arithmetic and copies ran while one was open for 63% -> 0% of each run, Pallas kernels for 0% -> 0%
where the time goes in v1:
time: 95.4 us; the launch traced here: 95.2 us
  Pallas kernels  90.4 us (95%)
  local copies, waits for them, and re-layouts  4.14 us (4%)
    pallas_call x1, Pallas kernels, per_device(): pl.pallas_call(kernel, out_shape=(jax.ShapeDtypeStruct((8, D, CHI), BF),...  90.4 us
    unnamed x2, local copies, waits for them, and re-layouts  2.54 us

profile of v1, /device:TPU:0, one launch (start us, length us, event | category | flops | bytes accessed | tf_op | source)
XLA Modules:
  0.0 95.2 jit_solution(7662047623116631559)
XLA Ops:
  0.6 90.4 %ctm_step.1 = (bf16[8,36,256]{2,1,0:T(8,128)(2,1)}, bf16[8,256]{1,0:T(8,128)(2,1)}, bf16[8,256]{1,0:T(8,128)(2,1)}) custom-call(bf16[256,256]{1,0:T(8,128)(2,1)} %bitcast.28, bf16[256,256]{1,0:T(8,128)(2,1)} %bitcast.29, bf16[36,8,256]{2,1,0:T(8,128)(2,1)} %bitcast.22, bf16[36,8,256]{2,1,0:T(8,128)(2,1)} %bitcast.23, bf16[36,8,256]{2,1,0:T(8,128)(2,1)} %bitcast.24, ...), custom_call_target="tpu_custom_call" | custom-call | tf_op jit(solution)/shard_map/ctm_step/pallas_call | solution.py:493
  91.0 1.6 %reshape.9 = bf16[1,288,256]{2,1,0:T(8,128)(2,1)} reshape(bf16[8,36,256]{2,1,0:T(8,128)(2,1)} %get-tuple-element.6) | data formatting | bytes 294912 | tf_op jit(solution)/shard_map/reshape | solution.py:508
  92.6 1.3 %copy.15 = bf16[1,8,256]{2,1,0:T(8,128)(2,1)} copy(bf16[1,8,256]{2,1,0:T(8,128)(2,1)} %bitcast.31) | data formatting | bytes 8192
  93.9 1.3 %copy.16 = bf16[1,8,256]{2,1,0:T(8,128)(2,1)} copy(bf16[1,8,256]{2,1,0:T(8,128)(2,1)} %bitcast.30) | data formatting | bytes 8192
